TPU v7x, 32 devices: a whole 2x2x4 slice. The times are simulated.
32 devices in a mesh: dp: 8 (over z, x), expert: 4 (over y, core).
Axes of the slice: x: 2, y: 2, z: 4, core: 2. Of those that a mesh axis runs over, the one named last changes fastest.
Arguments:
- tokens: bfloat16 [512, 2048], P('expert'), may hold values from -6 to 6
- cotangent: bfloat16 [512, 2048], P('expert'), may hold values from -0.75 to 0.75
- router_logits: float32 [512, 2], P('expert'), may hold values from -6 to 6
- routes: int32 [512, 2], P('expert'), may hold values from 0 to 3, all different within a row; in each aligned block of 128 rows (0 to 127, 128 to 255, ...) at most 96 rows name the same one
- gate_weight: bfloat16 [4, 7168, 2048], P('expert', 'dp'), may hold values from -0.125 to 0.125
- up_weight: bfloat16 [4, 7168, 2048], P('expert', 'dp'), may hold values from -0.125 to 0.125
- down_weight: bfloat16 [4, 7168, 2048], P('expert', 'dp'), may hold values from -0.0625 to 0.0625
- dir_gate: bfloat16 [4, 7168, 2048], P('expert', 'dp'), may hold values from -0.125 to 0.125
- dir_up: bfloat16 [4, 7168, 2048], P('expert', 'dp'), may hold values from -0.125 to 0.125
- dir_down: bfloat16 [4, 7168, 2048], P('expert', 'dp'), may hold values from -0.0625 to 0.0625
Outputs:
- mixed: bfloat16 [512, 2048], P('expert')
- hvp_gate: float32 [4, 7168, 2048], P('expert', 'dp')
- hvp_up: float32 [4, 7168, 2048], P('expert', 'dp')
- hvp_down: float32 [4, 7168, 2048], P('expert', 'dp')
Inputs may be any that keep to these rules, and one draw needn't show every extreme that they name: `routes`: each row names 2 different experts; among the 128 rows of one index of the expert axis no expert is named more than 96 times, and in every draw some block names some expert exactly 96 times.
All inputs are finite; a program needn't handle non-finite values.
Results may differ from a plain program's by a relative error of at most 0.0074.
Values may be sent and summed in bfloat16 or wider, within the bound.
A program may use at most 128 MiB of HBM per device.

v0:
```python
import jax
import jax.numpy as jnp
from jax import lax
from jax.sharding import PartitionSpec as P


def derivatives(preact):
    sigmoid_value = jax.nn.sigmoid(preact)
    slope_one = sigmoid_value * (1.0 + preact * (1.0 - sigmoid_value))
    slope_two = sigmoid_value * (1.0 - sigmoid_value) * (2.0 + preact * (1.0 - 2.0 * sigmoid_value))
    return (preact * sigmoid_value, slope_one, slope_two)


def project(left_rows, matrix):
    return jnp.einsum("rd,hd->rh", left_rows, matrix, preferred_element_type=jnp.float32)


def outer_sum(left_rows, right_rows):
    return jnp.einsum("rh,rd->hd", left_rows, right_rows, preferred_element_type=jnp.float32)


def block_terms(weights, token_rows, cot_rows):
    gate_mat, up_mat, down_mat, gate_dir, up_dir, down_dir = weights
    preact = project(token_rows, gate_mat)
    up_value = project(token_rows, up_mat)
    back_grad = project(cot_rows, down_mat)
    tang_gate = project(token_rows, gate_dir)
    tang_up = project(token_rows, up_dir)
    back_tang = project(cot_rows, down_dir)
    silu_value, slope_one, slope_two = derivatives(preact)
    hidden = (silu_value * up_value).astype(jnp.bfloat16)
    silu_tang = slope_one * tang_gate
    hidden_tang = (silu_tang * up_value + silu_value * tang_up).astype(jnp.bfloat16)
    resid_gate = (
        (back_tang * up_value + back_grad * tang_up) * slope_one
        + back_grad * up_value * slope_two * tang_gate
    ).astype(jnp.bfloat16)
    resid_up = (back_tang * silu_value + back_grad * silu_tang).astype(jnp.bfloat16)
    return (
        hidden,
        outer_sum(resid_gate, token_rows),
        outer_sum(resid_up, token_rows),
        outer_sum(hidden_tang, cot_rows),
    )


def shards(
    tokens,
    cotangent,
    router_logits,
    routes,
    gate_weight,
    up_weight,
    down_weight,
    dir_gate,
    dir_up,
    dir_down,
):
    tok_dev = tokens.shape[0]
    model_width = tokens.shape[1]
    top_count = routes.shape[1]
    experts = lax.axis_size("expert") * gate_weight.shape[0]
    capacity = top_count * tok_dev * 3 // (2 * experts)
    local_rows = experts * capacity
    weights = (gate_weight[0], up_weight[0], down_weight[0], dir_gate[0], dir_up[0], dir_down[0])
    gate_first = jax.nn.sigmoid(router_logits[:, 0] - router_logits[:, 1])
    gate_prob = jnp.stack([gate_first, 1.0 - gate_first], axis=1)
    flat_routes = routes.reshape(-1)
    onehot = (flat_routes[:, None] == jnp.arange(experts, dtype=jnp.int32)[None, :]).astype(
        jnp.int32
    )
    earlier = jnp.cumsum(onehot, axis=0) - onehot
    slot_pos = jnp.sum(earlier * onehot, axis=1)
    slot_index = flat_routes * capacity + slot_pos
    dispatch = (jnp.arange(local_rows, dtype=jnp.int32)[:, None] == slot_index[None, :]).astype(
        jnp.bfloat16
    )
    repeated = jnp.repeat(tokens, top_count, axis=0)
    scaled = (
        gate_prob.reshape(-1)[:, None]
        * jnp.repeat(cotangent, top_count, axis=0).astype(jnp.float32)
    ).astype(jnp.bfloat16)
    send_rows = (
        jnp.dot(dispatch, repeated, preferred_element_type=jnp.float32)
        .astype(jnp.bfloat16)
        .reshape(experts, capacity, model_width)
    )
    send_cot = (
        jnp.dot(dispatch, scaled, preferred_element_type=jnp.float32)
        .astype(jnp.bfloat16)
        .reshape(experts, capacity, model_width)
    )
    arrived_rows, arrived_cot = (
        lax.all_to_all(send_rows, "expert", split_axis=0, concat_axis=0, tiled=True),
        lax.all_to_all(send_cot, "expert", split_axis=0, concat_axis=0, tiled=True),
    )
    hidden, hvp_gate, hvp_up, hvp_down = block_terms(
        weights,
        arrived_rows.reshape(local_rows, model_width),
        arrived_cot.reshape(local_rows, model_width),
    )
    partial_out = jnp.dot(hidden, weights[2], preferred_element_type=jnp.float32)
    shares = lax.psum_scatter(partial_out, "dp", scatter_dimension=1, tiled=True)
    share_width = shares.shape[1]
    expert_out = shares.astype(jnp.bfloat16).reshape(experts, capacity, share_width)
    returned = lax.all_to_all(expert_out, "expert", split_axis=0, concat_axis=0, tiled=True)
    picked = jnp.dot(
        dispatch.T, returned.reshape(local_rows, share_width), preferred_element_type=jnp.float32
    ).reshape(tok_dev, top_count, share_width)
    mixed_share = jnp.sum(gate_prob[:, :, None] * picked, axis=1).astype(jnp.bfloat16)
    mixed = lax.all_gather(mixed_share, "dp", axis=1, tiled=True)
    return (mixed, hvp_gate[None], hvp_up[None], hvp_down[None])


def solution(mesh):
    in_specs = (
        P("expert", None),
        P("expert", None),
        P("expert", None),
        P("expert", None),
        P("expert", "dp", None),
        P("expert", "dp", None),
        P("expert", "dp", None),
        P("expert", "dp", None),
        P("expert", "dp", None),
        P("expert", "dp", None),
    )
    out_specs = (
        P("expert", None),
        P("expert", "dp", None),
        P("expert", "dp", None),
        P("expert", "dp", None),
    )
    return jax.shard_map(shards, mesh=mesh, in_specs=in_specs, out_specs=out_specs, check_vma=False)
```

profile of v0, /device:TPU:0, one launch (start us, length us, event | category | flops | bytes accessed | tf_op | source)
XLA Modules:
  0.0 173.9 jit_solution(14878815522278558503)
XLA Ops:
  7.2 0.0 reduce-scatter.2.cloned.1.call-start
  7.2 0.8 copy.16
  8.0 0.1 reshape.87
  8.1 0.1 eq.55
  8.3 1.2 reduce-window.6
  9.5 0.1 slice.16
  9.6 0.1 copy.18
  9.7 0.1 copy.19
  9.8 0.1 add_bitcast_fusion
  9.9 1.7 broadcast_in_dim.19
  11.6 0.4 reshape.89
  12.1 0.0 copy-start.9
  12.1 0.6 convolution_convert_fusion.1
  12.7 24.3 %all_to_all.15 = bf16[4,96,2048]{2,1,0:T(8,128)(2,1)S(1)} all-to-all(bf16[4,96,2048]{2,1,0:T(8,128)(2,1)S(1)} %bitcast.70), channel_id=1, replica_groups=mesh['dp'=8,'expert'=4] {'expert'}, dimensions={0} | all-to-all | bytes 3145728 | tf_op jit(solution)/shard_map/all_to_all | solution.py:94
  36.9 0.0 copy-start
  36.9 0.0 copy-done.9
  36.9 1.8 %fusion.12 = f32[384,896]{1,0:T(8,128)S(1)} fusion(bf16[384,2048]{1,0:T(8,128)(2,1)S(1)} %bitcast.64, bf16[1,896,2048]{2,1,0:T(8,128)(2,1)S(1)} %copy-done.9), kind=kOutput, calls=%fused_computation.15 | convolution fusion | flops 1409286144 | bytes 6619136 | tf_op jit(solution)/shard_map/rd,hd->rh/dot_general | solution.py:15
  38.8 0.0 copy-done
  38.8 0.8 copy-done.10
  39.5 1.8 %fusion.10 = f32[384,896]{1,0:T(8,128)S(1)} fusion(bf16[384,2048]{1,0:T(8,128)(2,1)S(1)} %bitcast.65, bf16[1,896,2048]{2,1,0:T(8,128)(2,1)S(1)} %copy-done.10), kind=kOutput, calls=%fused_computation.13 | convolution fusion | flops 1409286144 | bytes 6619136 | tf_op jit(solution)/shard_map/rd,hd->rh/dot_general | solution.py:15
  41.4 0.0 copy-start.3
  41.4 1.1 copy-done.3
  42.5 0.0 copy-done.12
  42.5 3.5 %fusion.8 = f32[384,2048]{1,0:T(8,128)} fusion(bf16[1,896,2048]{2,1,0:T(8,128)(2,1)S(1)} %copy-done.12, f32[384,896]{1,0:T(8,128)S(1)} %fusion.10, f32[384,896]{1,0:T(8,128)S(1)} %fusion.12), kind=kOutput, calls=%fused_computation.11 | convolution fusion | flops 1411350528 | bytes 9568256 | tf_op jit(solution)/shard_map/dot_general | solution.py:102
  46.0 0.0 reduce-scatter.2.cloned.1.call-update
  46.1 0.7 copy-done.8
  46.7 0.1 copy.21
  46.9 0.1 mul.95
  47.0 2.1 %broadcast_in_dim.20 = f32[128,2,2048]{2,1,0:T(2,128)S(1)} broadcast(bf16[128,2048]{1,0:T(8,128)(2,1)} %param.11), dimensions={0,2} | broadcast | bytes 2621440 | tf_op jit(solution)/shard_map/broadcast_in_dim | solution.py:81
  49.1 2.4 %convert_element_type.49 = f32[256,2048]{1,0:T(8,128)} reshape(f32[128,2,2048]{2,1,0:T(2,128)S(1)} %broadcast_in_dim.20) | data formatting | bytes 4194304 | tf_op jit(solution)/shard_map/convert_element_type | solution.py:81
  51.5 3.4 %convolution_convert_fusion = bf16[384,2048]{1,0:T(8,128)(2,1)} fusion(f32[256,2048]{1,0:T(8,128)} %convert_element_type.49, f32[256]{0:T(256)S(1)} %mul.95, s32[256]{0:T(256)S(1)} %multiply_add_fusion), kind=kOutput, calls=%fused_computation.17 | convolution fusion | flops 404586496 | bytes 3672064 | tf_op jit(solution)/shard_map/dot_general | solution.py:89
  54.9 4.5 %all-to-all-start.2 = ((bf16[4,96,2048]{2,1,0:T(8,128)(2,1)}), bf16[4,96,2048]{2,1,0:T(8,128)(2,1)}, u32[]{:S(2)}, u32[]{:S(2)}) async-start(bf16[4,96,2048]{2,1,0:T(8,128)(2,1)} %bitcast.10), calls=%async_computation.3 | async-start | bytes 3145728 | tf_op jit(solution)/shard_map/all_to_all | solution.py:95
  59.5 0.1 iota_compare_fusion.3
  59.6 0.1 eq.61
  59.7 0.0 copy-start.1
  59.7 0.0 copy-start.11
  59.7 4.5 %fusion = f32[384,896]{1,0:T(8,128)S(1)} fusion(bf16[384,2048]{1,0:T(8,128)(2,1)} %bitcast.66, bf16[1,896,2048]{2,1,0:T(8,128)(2,1)} %param.17), kind=kOutput, calls=%fused_computation.3 | convolution fusion | flops 1409286144 | bytes 6619136 | tf_op jit(solution)/shard_map/rd,hd->rh/dot_general | solution.py:15
  64.3 0.0 copy-done.1
  64.3 0.0 copy-done.11
  64.3 2.9 %fusion.2 = f32[384,896]{1,0:T(8,128)} fusion(bf16[384,2048]{1,0:T(8,128)(2,1)S(1)} %bitcast.68, bf16[1,896,2048]{2,1,0:T(8,128)(2,1)S(1)} %copy-done.11), kind=kOutput, calls=%fused_computation.5 | convolution fusion | flops 1409286144 | bytes 6619136 | tf_op jit(solution)/shard_map/rd,hd->rh/dot_general | solution.py:15
  67.2 12.2 %all-to-all-done.2 = bf16[4,96,2048]{2,1,0:T(8,128)(2,1)} async-done(((bf16[4,96,2048]{2,1,0:T(8,128)(2,1)}), bf16[4,96,2048]{2,1,0:T(8,128)(2,1)}, u32[]{:S(2)}, u32[]{:S(2)}) %all-to-all-start.2) | async-done | bytes 1572896 | tf_op jit(solution)/shard_map/all_to_all | solution.py:95
  79.4 4.5 %fusion.6 = f32[384,896]{1,0:T(8,128)S(1)} fusion(bf16[384,2048]{1,0:T(8,128)(2,1)} %bitcast.11, bf16[1,896,2048]{2,1,0:T(8,128)(2,1)} %param.16), kind=kOutput, calls=%fused_computation.9 | convolution fusion | flops 1409286144 | bytes 6619136 | tf_op jit(solution)/shard_map/rd,hd->rh/dot_general | solution.py:15
  84.0 0.0 copy-done.13
  84.0 0.0 copy-start.5
  84.0 0.0 copy-start.4
  84.0 0.0 copy-start.7
  84.0 3.7 %fusion.4 = f32[384,896]{1,0:T(8,128)S(1)} fusion(bf16[384,2048]{1,0:T(8,128)(2,1)} %bitcast.11, bf16[1,896,2048]{2,1,0:T(8,128)(2,1)S(1)} %copy-done.13), kind=kOutput, calls=%fused_computation.7 | convolution fusion | flops 1409286144 | bytes 6619136 | tf_op jit(solution)/shard_map/rd,hd->rh/dot_general | solution.py:15
  87.8 0.0 copy-done.4
  87.8 0.0 copy-done.7
  87.8 0.0 copy-start.6
  87.8 0.0 copy-start.2
  87.8 7.5 %convolution_bitcast_fusion = f32[1,896,2048]{2,1,0:T(8,128)} fusion(bf16[384,2048]{1,0:T(8,128)(2,1)} %bitcast.11, f32[384,896]{1,0:T(8,128)S(1)} %copy-done.7, f32[384,896]{1,0:T(8,128)S(1)} %copy-done.4, f32[384,896]{1,0:T(8,128)S(1)} %fusion, f32[384,896]{1,0:T(8,128)S(1)} %fusion.12), kind=kOutput, calls=%fused_computation | convolution fusion | flops 1413758976 | bytes 14417920 | tf_op jit(solution)/shard_map/rh,rd->hd/dot_general | solution.py:19
  95.3 0.0 copy-done.5
  95.3 0.0 copy-done.6
  95.3 0.0 copy-done.2
  95.3 5.8 %convolution_bitcast_fusion.2 = f32[1,896,2048]{2,1,0:T(8,128)} fusion(bf16[384,2048]{1,0:T(8,128)(2,1)S(1)} %bitcast.69, f32[384,896]{1,0:T(8,128)S(1)} %fusion, f32[384,896]{1,0:T(8,128)S(1)} %fusion.12, f32[384,896]{1,0:T(8,128)S(1)} %fusion.6, f32[384,896]{1,0:T(8,128)S(1)} %copy-done.4, f32[384,896]{1,0:T(8,128)S(1)} %copy-done.7, f32[384,896]{1,0:T(8,128)S(1)} %fusion.4), kind=kOutput, calls=%fused_computation.2 | convolution fusion | flops 1416855552 | bytes 17170432 | tf_op jit(solution)/shard_map/rh,rd->hd/dot_general | solution.py:19
  101.1 20.4 %reduce-scatter.2.cloned.1.call-done = f32[384,256]{1,0:T(8,128)} async-done(((f32[384,2048]{1,0:T(8,128)}), f32[384,256]{1,0:T(8,128)}) %reduce-scatter.2.cloned.1.call-update) | async-done | bytes 393232 | tf_op jit(solution)/shard_map/reduce_scatter | solution.py:103
  121.5 1.7 convert_element_type.46
  123.2 3.6 %all-to-all-start.1 = ((bf16[4,96,256]{2,1,0:T(8,128)(2,1)}), bf16[4,96,256]{2,1,0:T(8,128)(2,1)S(1)}, u32[]{:S(2)}, u32[]{:S(2)}) async-start(bf16[4,96,256]{2,1,0:T(8,128)(2,1)} %bitcast.7), calls=%async_computation.2 | async-start | bytes 393216 | tf_op jit(solution)/shard_map/all_to_all | solution.py:106
  126.8 7.8 %convolution_bitcast_fusion.1 = f32[1,896,2048]{2,1,0:T(8,128)} fusion(bf16[384,2048]{1,0:T(8,128)(2,1)} %bitcast.67, f32[384,896]{1,0:T(8,128)} %copy-done.5, f32[384,896]{1,0:T(8,128)} %copy-done.6, f32[384,896]{1,0:T(8,128)S(1)} %fusion, f32[384,896]{1,0:T(8,128)S(1)} %fusion.12), kind=kOutput, calls=%fused_computation.1 | convolution fusion | flops 1413758976 | bytes 14417920 | tf_op jit(solution)/shard_map/rh,rd->hd/dot_general | solution.py:19
  134.6 0.0 all-to-all-done.1
  134.6 0.2 fusion.22
  134.8 31.5 %all_gather.3 = bf16[128,2048]{1,0:T(8,128)(2,1)S(1)} all-gather(bf16[128,256]{1,0:T(8,128)(2,1)S(1)} %fusion.22), channel_id=1, replica_groups=mesh['dp'=8,'expert'=4] {'dp'}, dimensions={1}, use_global_device_ids=true | all-gather | bytes 589824 | tf_op jit(solution)/shard_map/all_gather | solution.py:111
  166.3 0.8 copy.27
  (11 shorter events, 0.1 us)
Async XLA Ops:
  7.2 114.3 %reduce-scatter.2.cloned.1.call-start = ((), (), s32[]{:S(2)}) async-start(), calls=%async_computation.4 | async-start | bytes 3538944 | tf_op jit(solution)/shard_map/reduce_scatter | solution.py:103
  12.1 24.9 %copy-start.9 = (bf16[1,896,2048]{2,1,0:T(8,128)(2,1)S(1)}, bf16[1,896,2048]{2,1,0:T(8,128)(2,1)}, u32[]{:S(2)}) copy-start(bf16[1,896,2048]{2,1,0:T(8,128)(2,1)} %param.14) | copy-start | bytes 11010052
  36.9 1.8 %copy-start = (bf16[4,96,2048]{2,1,0:T(8,128)(2,1)}, bf16[4,96,2048]{2,1,0:T(8,128)(2,1)S(1)}, u32[]{:S(2)}) copy-start(bf16[4,96,2048]{2,1,0:T(8,128)(2,1)S(1)} %all_to_all.15) | copy-start | bytes 4718596
  36.9 2.6 %copy-start.10 = (bf16[1,896,2048]{2,1,0:T(8,128)(2,1)S(1)}, bf16[1,896,2048]{2,1,0:T(8,128)(2,1)}, u32[]{:S(2)}) copy-start(bf16[1,896,2048]{2,1,0:T(8,128)(2,1)} %param.15) | copy-start | bytes 11010052
  39.5 3.0 %copy-start.12 = (bf16[1,896,2048]{2,1,0:T(8,128)(2,1)S(1)}, bf16[1,896,2048]{2,1,0:T(8,128)(2,1)}, u32[]{:S(2)}) copy-start(bf16[1,896,2048]{2,1,0:T(8,128)(2,1)} %param.16) | copy-start | bytes 11010052
  41.4 1.1 copy-start.3
  46.0 0.7 copy-start.8
  54.9 24.5 %all-to-all-start.2 = ((bf16[4,96,2048]{2,1,0:T(8,128)(2,1)}), bf16[4,96,2048]{2,1,0:T(8,128)(2,1)}, u32[]{:S(2)}, u32[]{:S(2)}) async-start(bf16[4,96,2048]{2,1,0:T(8,128)(2,1)} %bitcast.10), calls=%async_computation.3 | async-start | bytes 3145728 | tf_op jit(solution)/shard_map/all_to_all | solution.py:95
  59.7 4.6 %copy-start.1 = (bf16[4,96,2048]{2,1,0:T(8,128)(2,1)S(1)}, bf16[4,96,2048]{2,1,0:T(8,128)(2,1)}, u32[]{:S(2)}) copy-start(bf16[4,96,2048]{2,1,0:T(8,128)(2,1)} %copy-done) | copy-start | bytes 4718596
  59.7 4.6 %copy-start.11 = (bf16[1,896,2048]{2,1,0:T(8,128)(2,1)S(1)}, bf16[1,896,2048]{2,1,0:T(8,128)(2,1)}, u32[]{:S(2)}) copy-start(bf16[1,896,2048]{2,1,0:T(8,128)(2,1)} %param.18) | copy-start | bytes 11010052
  79.4 4.6 %copy-start.13 = (bf16[1,896,2048]{2,1,0:T(8,128)(2,1)S(1)}, bf16[1,896,2048]{2,1,0:T(8,128)(2,1)}, u32[]{:S(2)}) copy-start(bf16[1,896,2048]{2,1,0:T(8,128)(2,1)} %param.19) | copy-start | bytes 11010052
  84.0 11.3 %copy-start.5 = (f32[384,896]{1,0:T(8,128)}, f32[384,896]{1,0:T(8,128)S(1)}, u32[]{:S(2)}) copy-start(f32[384,896]{1,0:T(8,128)S(1)} %fusion.6) | copy-start | bytes 4128772
  84.0 3.8 %copy-start.4 = (f32[384,896]{1,0:T(8,128)S(1)}, f32[384,896]{1,0:T(8,128)}, u32[]{:S(2)}) copy-start(f32[384,896]{1,0:T(8,128)} %copy-done.3) | copy-start | bytes 4128772
  84.0 3.8 %copy-start.7 = (f32[384,896]{1,0:T(8,128)S(1)}, f32[384,896]{1,0:T(8,128)}, u32[]{:S(2)}) copy-start(f32[384,896]{1,0:T(8,128)} %fusion.2) | copy-start | bytes 4128772
  87.8 7.5 %copy-start.6 = (f32[384,896]{1,0:T(8,128)}, f32[384,896]{1,0:T(8,128)S(1)}, u32[]{:S(2)}) copy-start(f32[384,896]{1,0:T(8,128)S(1)} %fusion.4) | copy-start | bytes 4128772
  87.8 7.5 %copy-start.2 = (bf16[4,96,2048]{2,1,0:T(8,128)(2,1)S(1)}, bf16[4,96,2048]{2,1,0:T(8,128)(2,1)}, u32[]{:S(2)}) copy-start(bf16[4,96,2048]{2,1,0:T(8,128)(2,1)} %copy-done) | copy-start | bytes 4718596
  123.2 11.4 %all-to-all-start.1 = ((bf16[4,96,256]{2,1,0:T(8,128)(2,1)}), bf16[4,96,256]{2,1,0:T(8,128)(2,1)S(1)}, u32[]{:S(2)}, u32[]{:S(2)}) async-start(bf16[4,96,256]{2,1,0:T(8,128)(2,1)} %bitcast.7), calls=%async_computation.2 | async-start | bytes 393216 | tf_op jit(solution)/shard_map/all_to_all | solution.py:106
Sparse Core Ops, SparseCore 0:
  46.2 75.2 reduce-scatter.1
where the time goes:
time: 175 us; the launch traced here: 174 us
  blocking collectives  55.8 us (32%)
  matrix products  48.1 us (27%)
  waiting for transfers between devices  32.6 us (19%)
  between operations  14.3 us (8%)
  local copies, waits for them, and re-layouts  11.7 us (7%)
  starting transfers between devices  8.16 us (5%)
  other arithmetic  3.2 us (2%)
    all_gather x1, blocking collectives, shards(): mixed = lax.all_gather(mixed_share, 'dp', axis=1, tiled=True)  31.5 us
    all_to_all x1, blocking collectives, shards(): lax.all_to_all(send_rows, 'expert', split_axis=0, concat_axis=0, tiled=True)  24.3 us
    dot_general x3, matrix products, outer_sum(): jnp.einsum('rh,rd->hd', left_rows, right_rows, preferred_element_type=jnp...  21 us
    reduce_scatter x1, waiting for transfers between devices, shards(): lax.psum_scatter(partial_out, 'dp', scatter_dimension=1, tiled=True)  20.4 us
    dot_general x6, matrix products, project(): jnp.einsum('rd,hd->rh', left_rows, matrix, preferred_element_type=jnp.flo...  19.4 us
    all_to_all x1, waiting for transfers between devices, shards(): lax.all_to_all(send_cot, 'expert', split_axis=0, concat_axis=0, tiled=True)  12.2 us
    all_to_all x1, starting transfers between devices, shards(): lax.all_to_all(send_cot, 'expert', split_axis=0, concat_axis=0, tiled=True)  4.54 us
    unnamed x30, local copies, waits for them, and re-layouts  4.17 us
  transfers between devices with their start and end apart: 3, of which 2 were waited for; matrix products, arithmetic and copies ran while one was open for 26% of the time, Pallas kernels for 0%

commit v1 on v0

v1 whole, which is shorter than its diff:
```python
import functools

import jax
import jax.numpy as jnp
from jax import lax
from jax.experimental import pallas as pl
from jax.experimental.pallas import tpu as pltpu
from jax.sharding import PartitionSpec as P

CHUNKS = 4
MESH = pl.DeviceIdType.MESH
VMEM = pl.BlockSpec(memory_space=pltpu.VMEM)


def meet(peers):
    barrier = pltpu.get_barrier_semaphore()
    for peer in peers:
        pl.semaphore_signal(barrier, inc=1, device_id=peer, device_id_type=MESH)
    pl.semaphore_wait(barrier, len(peers))


def send(src, dst, sems, slot, peer):
    send_sems, recv_sems = sems
    return pltpu.make_async_remote_copy(
        src_ref=src,
        dst_ref=dst,
        send_sem=send_sems.at[slot],
        recv_sem=recv_sems.at[slot],
        device_id=peer,
        device_id_type=MESH,
    )


def gather_kernel(
    chips, tok_ref, cot_ref, gate_ref, all_tok, all_cot, all_gate, *sems
):
    row, col = lax.axis_index("dp"), lax.axis_index("expert")
    chip, core = col // 2, col % 2
    side = row % 2
    other_row = row + 1 - 2 * side
    partner_col = col + 1 - 2 * core
    partner, beside = (row, partner_col), (other_row, col)
    experts = 2 * chips
    others = [(row, lax.rem(col + step, experts)) for step in range(1, experts)]
    meet(others + [beside])
    own, meta, far, near, relay = (sems[2 * i : 2 * i + 2] for i in range(5))
    half = tok_ref.shape[0] // 2
    part = half // CHUNKS
    pairs = ((tok_ref, all_tok), (cot_ref, all_cot))
    started = []
    arrivals = []

    for chunk in range(CHUNKS):
        for step in range(1, chips):
            peer = (row, lax.rem(chip + step, chips) * 2 + core)
            for which, (src, dst) in enumerate(pairs):
                rows = pl.ds(pl.multiple_of(side * half + chunk * part, part), part)
                slot = ((step - 1) * CHUNKS + chunk) * 2 + which
                copy = send(src.at[rows], dst.at[col, rows], far, slot, peer)
                copy.start()
                started.append(copy)
    for step, peer in enumerate(others):
        copy = send(gate_ref, all_gate.at[col], meta, step, peer)
        copy.start()
        started.append(copy)
        arrivals.append(copy)
    for which, (src, dst) in enumerate(pairs):
        copy = send(src, dst.at[col], own, which, partner)
        copy.start()
        started.append(copy)
        arrivals.append(copy)
    all_tok[pl.ds(col, 1)] = tok_ref[...][None]
    all_cot[pl.ds(col, 1)] = cot_ref[...][None]
    all_gate[pl.ds(col, 1)] = gate_ref[...][None]

    def pass_on(dst, block, rows, slot, source, both):
        send(dst.at[block, rows], dst.at[block, rows], source, slot, partner).wait_recv()
        index = slot * 2 + (0 if both else 1)
        onward = send(dst.at[block, rows], dst.at[block, rows], relay, index, partner)
        if both:
            across = send(dst.at[block, rows], dst.at[block, rows], near, slot, beside)
            across.start()
            started.append(across)
        onward.start()
        started.append(onward)
        arrivals.append(onward)

    for source, both, lag in ((far, True, 0), (near, False, 0)):
        for chunk in range(CHUNKS):
            for step in range(1, chips):
                block = lax.rem(chip + chips - step, chips) * 2 + core
                from_side = side if both else 1 - side
                rows = pl.ds(pl.multiple_of(from_side * half + chunk * part, part), part)
                for which, (_, dst) in enumerate(pairs):
                    slot = ((step - 1) * CHUNKS + chunk) * 2 + which
                    pass_on(dst, block, rows, slot, source, both)
    for copy in arrivals:
        copy.wait_recv()
    for copy in started:
        copy.wait_send()


def gather_blocks(tokens, cotangent, gates, chips):
    slots = max(1, (chips - 1) * CHUNKS * 2)
    experts = 2 * chips
    dma = pltpu.SemaphoreType.DMA
    counts = (2, experts - 1, slots, slots, 2 * slots)
    blocks = (experts,) + tokens.shape
    return pl.pallas_call(
        functools.partial(gather_kernel, chips),
        out_shape=(
            jax.ShapeDtypeStruct(blocks, tokens.dtype),
            jax.ShapeDtypeStruct(blocks, cotangent.dtype),
            jax.ShapeDtypeStruct((experts,) + gates.shape, gates.dtype),
        ),
        in_specs=[VMEM] * 3,
        out_specs=(VMEM,) * 3,
        scratch_shapes=[dma((count,)) for count in counts for _ in range(2)],
        compiler_params=pltpu.CompilerParams(
            collective_id=0, has_side_effects=True, vmem_limit_bytes=60 * 2**20
        ),
        name="gather_blocks",
    )(tokens, cotangent, gates)


def across(left, right):
    return lax.dot_general(left, right, (((1,), (1,)), ((), ())), preferred_element_type=jnp.float32)


def block_kernel(
    tok_ref, cot_ref, gate_ref, g_ref, u_ref, w_ref, vg_ref, vu_ref, vw_ref,
    hvp_g, hvp_u, hvp_w, out_ref, scaled, total,
):
    step = pl.program_id(0)

    @pl.when(step == 0)
    def _():
        scaled[...] = (gate_ref[...] * cot_ref[...].astype(jnp.float32)).astype(jnp.bfloat16)
        total[...] = jnp.zeros_like(total)

    tok, cot = tok_ref[...], scaled[...]
    a, b = across(g_ref[...], tok), across(u_ref[...], tok)
    ta, tb = across(vg_ref[...], tok), across(vu_ref[...], tok)
    q, tq = across(w_ref[...], cot), across(vw_ref[...], cot)
    s = jax.nn.sigmoid(a)
    g = a * s
    g1 = s * (1.0 + a * (1.0 - s))
    g2 = s * (1.0 - s) * (2.0 + a * (1.0 - 2.0 * s))
    tg = g1 * ta
    hidden = (g * b).astype(jnp.bfloat16)
    hidden_tang = (tg * b + g * tb).astype(jnp.bfloat16)
    resid_gate = ((tq * b + q * tb) * g1 + q * b * g2 * ta).astype(jnp.bfloat16)
    resid_up = (tq * g + q * tg).astype(jnp.bfloat16)
    total[...] += lax.dot_general(
        hidden, w_ref[...], (((0,), (0,)), ((), ())), preferred_element_type=jnp.float32
    )
    hvp_g[...] = jnp.dot(resid_gate, tok, preferred_element_type=jnp.float32)
    hvp_u[...] = jnp.dot(resid_up, tok, preferred_element_type=jnp.float32)
    hvp_w[...] = jnp.dot(hidden_tang, cot, preferred_element_type=jnp.float32)

    @pl.when(step == pl.num_programs(0) - 1)
    def _():
        out_ref[...] = (gate_ref[...] * total[...]).astype(jnp.bfloat16)


def block_terms(tokens, cotangent, gate, weights):
    rows, width = tokens.shape
    units = weights[0].shape[0]
    tile = max(n for n in range(16, units + 1, 16) if units % n == 0 and n * rows <= 224 * 512)
    whole = lambda shape: pl.BlockSpec(shape, lambda i: (0, 0))
    piece = pl.BlockSpec((tile, width), lambda i: (i, 0))
    out = jax.ShapeDtypeStruct((units, width), jnp.float32)
    return pl.pallas_call(
        block_kernel,
        grid=(units // tile,),
        out_shape=(out, out, out, jax.ShapeDtypeStruct((rows, width), jnp.bfloat16)),
        in_specs=[whole((rows, width)), whole((rows, width)), whole((rows, 1))] + [piece] * 6,
        out_specs=(piece, piece, piece, whole((rows, width))),
        scratch_shapes=[
            pltpu.VMEM((rows, width), jnp.bfloat16),
            pltpu.VMEM((rows, width), jnp.float32),
        ],
        compiler_params=pltpu.CompilerParams(
            dimension_semantics=("arbitrary",), vmem_limit_bytes=63 * 2**20
        ),
        name="block_terms",
    )(tokens, cotangent, gate, *weights)


def combine_kernel(
    chips, layers, part_ref, out_ref,
    from_core, core_sum, y_first, a_sum, x_last, x_first, b_sum, y_last, plane, from_z, share,
    gathered, from_partner, *sems,
):
    row, col = lax.axis_index("dp"), lax.axis_index("expert")
    chip, core = col // 2, col % 2
    layer, side = row // 2, row % 2
    partner = (row, col + 1 - 2 * core)
    beside = (row + 1 - 2 * side, col)
    chip_peers = [(row, lax.rem(chip + n, chips) * 2 + core) for n in range(1, chips)]
    layer_peers = [(lax.rem(layer + n, layers) * 2 + side, col) for n in range(1, layers)]
    meet([partner, beside] + chip_peers + layer_peers)
    core_s, ya_s, xa_s, xb_s, yb_s, z_s, gz_s, gx_s, back_s = (sems[2 * i : 2 * i + 2] for i in range(9))
    width = part_ref.shape[1]
    feats = width // 2
    wide, slim = feats // 2, feats // 4
    chip_rows = part_ref.shape[0] // chips
    rows_z = chip_rows // layers
    tok_dev = chip_rows // 2
    f32, bf16 = jnp.float32, jnp.bfloat16
    sent = []

    def go(src, dst, sems, slot, peer):
        copy = send(src, dst, sems, slot, peer)
        copy.start()
        sent.append(copy)
        return copy

    def cols(start, size):
        return pl.ds(pl.multiple_of(start, size), size)

    mine, theirs = cols(core * feats, feats), cols((1 - core) * feats, feats)
    my_slim, their_slim = cols(side * slim, slim), cols((1 - side) * slim, slim)
    my_rows = cols(chip * chip_rows, chip_rows)

    go(part_ref.at[:, theirs], from_core, core_s, 0, partner).wait_recv()
    core_sum[...] = (part_ref[:, mine].astype(f32) + from_core[...].astype(f32)).astype(bf16)

    late = wide + (1 - side) * slim
    x_copy = go(core_sum.at[:, cols(late, slim)], x_first, xb_s, 0, beside)
    y_copies = []
    for n, peer in enumerate(chip_peers):
        target = lax.rem(chip + n + 1, chips)
        source = core_sum.at[cols(target * chip_rows, chip_rows), pl.ds(0, wide)]
        y_copies.append(go(source, y_first.at[n], ya_s, n, peer))
    value = core_sum[my_rows, :wide].astype(f32)
    for n, copy in enumerate(y_copies):
        copy.wait_recv()
        value = value + y_first[n].astype(f32)
    a_sum[...] = value.astype(bf16)
    x_last_copy = go(a_sum.at[:, their_slim], x_last, xa_s, 0, beside)
    x_copy.wait_recv()
    b_sum[...] = (
        core_sum[:, cols(wide + side * slim, slim)].astype(f32) + x_first[...].astype(f32)
    ).astype(bf16)
    y_copies = []
    for n, peer in enumerate(chip_peers):
        target = lax.rem(chip + n + 1, chips)
        source = b_sum.at[cols(target * chip_rows, chip_rows)]
        y_copies.append(go(source, y_last.at[n], yb_s, n, peer))
    x_last_copy.wait_recv()
    plane[:, :slim] = (a_sum[:, my_slim].astype(f32) + x_last[...].astype(f32)).astype(bf16)
    value = b_sum[my_rows].astype(f32)
    for n, copy in enumerate(y_copies):
        copy.wait_recv()
        value = value + y_last[n].astype(f32)
    plane[:, slim:] = value.astype(bf16)

    z_copies = []
    for n, peer in enumerate(layer_peers):
        target = lax.rem(layer + n + 1, layers)
        z_copies.append(go(plane.at[cols(target * rows_z, rows_z)], from_z.at[n], z_s, n, peer))
    my_z = cols(layer * rows_z, rows_z)
    value = plane[my_z].astype(f32)
    for n, copy in enumerate(z_copies):
        copy.wait_recv()
        value = value + from_z[n].astype(f32)
    share[...] = value.astype(bf16)

    x_back = [go(share, gathered.at[side, my_z], gx_s, 0, beside)]
    z_back = []
    for n, peer in enumerate(layer_peers):
        z_back.append(go(share, gathered.at[side, my_z], gz_s, n, peer))
    gathered[pl.ds(side, 1), my_z] = share[...][None]
    for n, copy in enumerate(z_back):
        copy.wait_recv()
        origin = lax.rem(layer + layers - n - 1, layers)
        place = gathered.at[side, cols(origin * rows_z, rows_z)]
        x_back.append(go(place, place, gx_s, n + 1, beside))
    own_block, partner_block = cols(core * tok_dev, tok_dev), cols((1 - core) * tok_dev, tok_dev)
    back = [go(gathered.at[side, partner_block], from_partner.at[side], back_s, 0, partner)]
    for copy in x_back:
        copy.wait_recv()
    back.append(go(gathered.at[1 - side, partner_block], from_partner.at[1 - side], back_s, 1, partner))
    for group in range(2):
        for half in range(2):
            at = cols(core * feats + group * wide + half * slim, slim)
            out_ref[:, at] = gathered[half, own_block, group * slim : (group + 1) * slim]
    for copy in back:
        copy.wait_recv()
    for group in range(2):
        for half in range(2):
            at = cols((1 - core) * feats + group * wide + half * slim, slim)
            out_ref[:, at] = from_partner[half, :, group * slim : (group + 1) * slim]
    for copy in sent:
        copy.wait_send()


def combine(part, chips, layers):
    rows, width = part.shape
    feats = width // 2
    wide, slim = feats // 2, feats // 4
    chip_rows = rows // chips
    rows_z = chip_rows // layers
    tok_dev = chip_rows // 2
    dma = pltpu.SemaphoreType.DMA
    far, deep = max(1, chips - 1), max(1, layers - 1)
    counts = (1, far, 1, 1, far, deep, deep, layers, 2)
    held = lambda *shape: pltpu.VMEM(shape, jnp.bfloat16)
    return pl.pallas_call(
        functools.partial(combine_kernel, chips, layers),
        out_shape=jax.ShapeDtypeStruct((tok_dev, width), jnp.bfloat16),
        in_specs=[VMEM],
        out_specs=VMEM,
        scratch_shapes=[
            held(rows, feats),
            held(rows, feats),
            held(far, chip_rows, wide),
            held(chip_rows, wide),
            held(chip_rows, slim),
            held(rows, slim),
            held(rows, slim),
            held(far, chip_rows, slim),
            held(chip_rows, wide),
            held(deep, rows_z, wide),
            held(rows_z, wide),
            held(2, chip_rows, wide),
            held(2, tok_dev, wide),
        ]
        + [dma((count,)) for count in counts for _ in range(2)],
        compiler_params=pltpu.CompilerParams(
            collective_id=1, has_side_effects=True, vmem_limit_bytes=60 * 2**20
        ),
        name="combine",
    )(part)


def shards(tokens, cotangent, router_logits, routes, *weights):
    experts = lax.axis_size("expert")
    chips, layers = experts // 2, lax.axis_size("dp") // 2
    tok_dev, width = tokens.shape
    lines = -(-experts // 8) * 8
    logits, named = router_logits.T, routes.T
    first = jax.nn.sigmoid(logits[0] - logits[1])[None]
    number = jnp.arange(lines, dtype=jnp.int32)[:, None]
    gates = jnp.where(named[0][None] == number, first, 0.0) + jnp.where(
        named[1][None] == number, 1.0 - first, 0.0
    )
    all_tok, all_cot, all_gate = gather_blocks(tokens, cotangent, gates, chips)
    rows = experts * tok_dev
    own = lax.dynamic_index_in_dim(all_gate, lax.axis_index("expert"), 1, keepdims=False)
    hvp_gate, hvp_up, hvp_down, part = block_terms(
        all_tok.reshape(rows, width),
        all_cot.reshape(rows, width),
        own.reshape(rows, 1),
        [weight[0] for weight in weights],
    )
    mixed = combine(part, chips, layers)
    return (mixed, hvp_gate[None], hvp_up[None], hvp_down[None])


def solution(mesh):
    rows, units = P("expert", None), P("expert", "dp", None)
    return jax.shard_map(
        shards,
        mesh=mesh,
        in_specs=(rows,) * 4 + (units,) * 6,
        out_specs=(rows, units, units, units),
        check_vma=False,
    )
```

time: 175 us -> 103 us (0.59)
  Pallas kernels: 0 us -> 96.2 us
  blocking collectives: 55.8 us -> 0 us
  matrix products: 48.1 us -> 0 us
  waiting for transfers between devices: 32.6 us -> 0 us
  between operations: 14.3 us -> 0.66 us
  starting transfers between devices: 8.16 us -> 0 us
  local copies, waits for them, and re-layouts: 11.7 us -> 4.24 us
  other arithmetic: 3.2 us -> 1.36 us
    pallas_call x0 -> x3, Pallas kernels: none -> 96.2 us  [the longest x1 38.5 us: combine(): pl.pallas_call(functools.partial(combine_kernel, chips, layers), out_shap...]
    dot_general x13 -> x0, matrix products: 48.1 us -> none  [the longest x3 21 us: outer_sum(): jnp.einsum('rh,rd->hd', left_rows, right_rows, preferred_element_type=jnp...]
    all_gather x1 -> x0, blocking collectives: 31.5 us -> none  [shards(): mixed = lax.all_gather(mixed_share, 'dp', axis=1, tiled=True)]
    all_to_all x1 -> x0, blocking collectives: 24.3 us -> none  [shards(): lax.all_to_all(send_rows, 'expert', split_axis=0, concat_axis=0, tiled=True)]
    reduce_scatter x1 -> x0, waiting for transfers between devices: 20.4 us -> none  [shards(): lax.psum_scatter(partial_out, 'dp', scatter_dimension=1, tiled=True)]
    all_to_all x2 -> x0, waiting for transfers between devices: 12.2 us -> none  [the longest x1 12.2 us: shards(): lax.all_to_all(send_cot, 'expert', split_axis=0, concat_axis=0, tiled=True)]
    all_to_all x2 -> x0, starting transfers between devices: 8.12 us -> none  [the longest x1 4.54 us: shards(): lax.all_to_all(send_cot, 'expert', split_axis=0, concat_axis=0, tiled=True)]
    broadcast_in_dim x2 -> x0, local copies, waits for them, and re-layouts: 3.76 us -> none  [the longest x1 2.09 us: shards(): jnp.repeat(cotangent, top_count, axis=0).astype(jnp.float32)]
  transfers between devices with their start and end apart: 3 -> 0, of which waited for: 2 -> 0; matrix products, arithmetic and copies ran while one was open for 26% -> 0% of each run, Pallas kernels for 0% -> 0%
where the time goes in v1:
time: 103 us; the launch traced here: 102 us
  Pallas kernels  96.2 us (93%)
  local copies, waits for them, and re-layouts  4.24 us (4%)
  other arithmetic  1.36 us (1%)
    pallas_call x1, Pallas kernels, combine(): pl.pallas_call(functools.partial(combine_kernel, chips, layers), out_shap...  38.5 us
    pallas_call x1, Pallas kernels, block_terms(): pl.pallas_call(block_kernel, grid=(units // tile,), out_shape=(out, out,...  33.3 us
    pallas_call x1, Pallas kernels, gather_blocks(): pl.pallas_call(functools.partial(gather_kernel, chips), out_shape=(jax.Sh...  24.4 us

profile of v1, /device:TPU:0, one launch (start us, length us, event | category | flops | bytes accessed | tf_op | source)
XLA Modules:
  0.0 102.4 jit_solution(1422842356213634520)
XLA Ops:
  0.6 0.8 subtract_bitcast_fusion
  1.4 0.8 slice_bitcast_fusion.1
  2.2 0.6 select_add_fusion.gate_ref
  2.8 24.4 %gather_blocks.1 = (bf16[4,128,2048]{2,1,0:T(8,128)(2,1)}, bf16[4,128,2048]{2,1,0:T(8,128)(2,1)}, f32[4,8,128]{2,1,0:T(8,128)}) custom-call(bf16[128,2048]{1,0:T(8,128)(2,1)} %tok_ref.1, bf16[128,2048]{1,0:T(8,128)(2,1)} %cot_ref.1, f32[8,128]{1,0:T(8,128)} %select_add_fusion.gate_ref), custom_call_target="tpu_custom_call" | custom-call | tf_op jit(solution)/shard_map/gather_blocks/pallas_call | solution.py:109
  27.2 0.7 dynamic-slice_bitcast_fusion
  27.9 0.9 copy.14.gate_ref
  28.8 33.3 %block_terms.1 = (f32[896,2048]{1,0:T(8,128)}, f32[896,2048]{1,0:T(8,128)}, f32[896,2048]{1,0:T(8,128)}, bf16[512,2048]{1,0:T(8,128)(2,1)}) custom-call(bf16[512,2048]{1,0:T(8,128)(2,1)} %bitcast.28, bf16[512,2048]{1,0:T(8,128)(2,1)} %bitcast.29, f32[512,1]{1,0:T(8,128)} %copy.14.gate_ref, bf16[896,2048]{1,0:T(8,128)(2,1)} %bitcast.22, ...), custom_call_target="tpu_custom_call" | custom-call | tf_op jit(solution)/shard_map/block_terms/pallas_call | solution.py:173
  62.1 38.5 %combine.1 = bf16[128,2048]{1,0:T(8,128)(2,1)} custom-call(bf16[512,2048]{1,0:T(8,128)(2,1)} %get-tuple-element.14.part_ref), custom_call_target="tpu_custom_call" | custom-call | tf_op jit(solution)/shard_map/combine/pallas_call | solution.py:310
  100.6 1.9 %copy.16 = bf16[128,2048]{1,0:T(8,128)(2,1)} copy(bf16[128,2048]{1,0:T(8,128)(2,1)} %combine.1) | data formatting | bytes 1048576

commit v2 on v1

--- a/solution.py
+++ b/solution.py
@@ -139,9 +139,9 @@
         total[...] = jnp.zeros_like(total)
 
     tok, cot = tok_ref[...], scaled[...]
-    a, b = across(g_ref[...], tok), across(u_ref[...], tok)
-    ta, tb = across(vg_ref[...], tok), across(vu_ref[...], tok)
-    q, tq = across(w_ref[...], cot), across(vw_ref[...], cot)
+    stacked = jnp.concatenate([g_ref[...], u_ref[...], vg_ref[...], vu_ref[...]], axis=0)
+    a, b, ta, tb = jnp.split(across(stacked, tok), 4, axis=0)
+    q, tq = jnp.split(across(jnp.concatenate([w_ref[...], vw_ref[...]], axis=0), cot), 2, axis=0)
     s = jax.nn.sigmoid(a)
     g = a * s
     g1 = s * (1.0 + a * (1.0 - s))

time: 103 us -> 99.8 us (0.969)
  Pallas kernels: 96.2 us -> 93.2 us
    pallas_call x1, Pallas kernels: 33.3 us -> 30.3 us  [block_terms(): pl.pallas_call(block_kernel, grid=(units // tile,), out_shape=(out, out,...]
where the time goes in v2:
time: 99.8 us; the launch traced here: 99.4 us
  Pallas kernels  93.2 us (93%)
  local copies, waits for them, and re-layouts  4.24 us (4%)
  other arithmetic  1.36 us (1%)
    pallas_call x1, Pallas kernels, combine(): pl.pallas_call(functools.partial(combine_kernel, chips, layers), out_shap...  38.5 us
    pallas_call x1, Pallas kernels, block_terms(): pl.pallas_call(block_kernel, grid=(units // tile,), out_shape=(out, out,...  30.3 us
    pallas_call x1, Pallas kernels, gather_blocks(): pl.pallas_call(functools.partial(gather_kernel, chips), out_shape=(jax.Sh...  24.4 us

profile of v2, /device:TPU:0, one launch (start us, length us, event | category | flops | bytes accessed | tf_op | source)
XLA Modules:
  0.0 99.4 jit_solution(1077445331932293660)
XLA Ops:
  0.6 0.8 subtract_bitcast_fusion
  1.4 0.8 slice_bitcast_fusion.1
  2.2 0.6 select_add_fusion.gate_ref
  2.8 24.4 %gather_blocks.1 = (bf16[4,128,2048]{2,1,0:T(8,128)(2,1)}, bf16[4,128,2048]{2,1,0:T(8,128)(2,1)}, f32[4,8,128]{2,1,0:T(8,128)}) custom-call(bf16[128,2048]{1,0:T(8,128)(2,1)} %tok_ref.1, bf16[128,2048]{1,0:T(8,128)(2,1)} %cot_ref.1, f32[8,128]{1,0:T(8,128)} %select_add_fusion.gate_ref), custom_call_target="tpu_custom_call" | custom-call | tf_op jit(solution)/shard_map/gather_blocks/pallas_call | solution.py:109
  27.2 0.7 dynamic-slice_bitcast_fusion
  27.9 0.9 copy.14.gate_ref
  28.8 30.3 %block_terms.1 = (f32[896,2048]{1,0:T(8,128)}, f32[896,2048]{1,0:T(8,128)}, f32[896,2048]{1,0:T(8,128)}, bf16[512,2048]{1,0:T(8,128)(2,1)}) custom-call(bf16[512,2048]{1,0:T(8,128)(2,1)} %bitcast.28, bf16[512,2048]{1,0:T(8,128)(2,1)} %bitcast.29, f32[512,1]{1,0:T(8,128)} %copy.14.gate_ref, bf16[896,2048]{1,0:T(8,128)(2,1)} %bitcast.22, ...), custom_call_target="tpu_custom_call" | custom-call | tf_op jit(solution)/shard_map/block_terms/pallas_call | solution.py:173
  59.1 38.5 %combine.1 = bf16[128,2048]{1,0:T(8,128)(2,1)} custom-call(bf16[512,2048]{1,0:T(8,128)(2,1)} %get-tuple-element.14.part_ref), custom_call_target="tpu_custom_call" | custom-call | tf_op jit(solution)/shard_map/combine/pallas_call | solution.py:310
  97.6 1.9 %copy.16 = bf16[128,2048]{1,0:T(8,128)(2,1)} copy(bf16[128,2048]{1,0:T(8,128)(2,1)} %combine.1) | data formatting | bytes 1048576
